TPU v7x, 512 devices: a whole 4x8x8 slice. The times are simulated.
512 devices in a mesh: blk: 64 (over x, y, core), phe: 8 (over z).
Axes of the slice: x: 4, y: 8, z: 8, core: 2. Of those that a mesh axis runs over, the one named last changes fastest.
Arguments:
- ld_rows: bfloat16 [65536, 1024], P('blk'), may hold values from -1.5 to 1.5, as said below
- block_first: int32 [65536], P('blk'), may hold values from 0 to 65535, as said below
- beta_hat: float32 [512, 65536], P('phe', 'blk'), may hold values from -6 to 6
- psi: float32 [512, 65536], P('phe', 'blk'), may hold values from 0.05 to 5
- noise: bfloat16 [3, 512, 65536], P(None, 'phe', 'blk'), may hold values from -5 to 5
- sample_size: int32 [512], P('phe'), may hold values from 2000 to 199999
Outputs:
- effects: float32 [512, 65536], P('phe', 'blk')
Inputs may be any that keep to these rules, and one draw needn't show every extreme that they name: block_first[j] is the first SNP of the run of consecutive SNPs that forms j's LD block; every block holds 128 to 1024 SNPs, except the last block, which ends at SNP 65536 - 1 and may hold fewer. ld_rows[j, c] is the LD between SNP j and SNP block_first[j] + c for c below the length of j's block, and zero for larger c; every block's matrix is symmetric with unit diagonal.
All inputs are finite; a program needn't handle non-finite values.
Results may differ from a plain program's by a relative error of at most 0.00055.
The roundings to bfloat16 on the way count: a program that leaves them out, or rounds other values in their place, can miss the bound.
Values may be sent and summed in bfloat16 or wider, within the bound.
A program may use at most 64 MiB of HBM per device.

v0:
```python
import functools

import jax
import jax.numpy as jnp
from jax import lax
from jax.experimental import pallas as pl
from jax.experimental.pallas import tpu as pltpu
from jax.sharding import PartitionSpec as P

ITERS = 3
TINY = 1e-06
SAMPLE_REF = 20000.0
MESH = pl.DeviceIdType.MESH
LANES = 128
NB = 8
CH = 256
NCH = 4
F32 = jnp.float32
BF16 = jnp.bfloat16
EARLY = True


def peer_offsets(nx, ny):
    def hops(d):
        dx, dy, dc = d
        return min(dx, nx - dx) + min(dy, ny - dy) + 0.2 * dc

    every = [(dx, dy, dc) for dx in range(nx) for dy in range(ny) for dc in range(2)]
    return sorted([d for d in every if d != (0, 0, 0)], key=lambda d: -hops(d))


def kernel(
    nx, ny, nz, snps,
    ld_hbm, bf_hbm, bfr_hbm, bh_hbm, psi_hbm, nz_hbm, ss_hbm,
    out_ref,
    ld_v, bf_s, bf_v, bh_v, psi_v, nz_v, ss_v,
    rt_m, x_v, acc_v, tail_v, beta_v, sh_v, u_v, v_v,
    low_v, lowl_v, lowr_v, t_v, tl_v, tr_v, psil_v, psir_v, nzl_v, nzr_v, shl_v, shr_v,
    rbuf, sbuf, pbuf,
    in_sem, rs_sem, rr_sem, ss_sem, sr_sem, ps_sem, pr_sem,
    ls_sem, lr_sem, qs_sem, qr_sem, ts_sem, tr_sem, ws_sem, wr_sem, hs_sem, hr_sem,
):
    nblk = nx * ny * 2
    me = lax.axis_index("blk")
    mz = lax.axis_index("phe")
    mx, my, mc = me // (2 * ny), (me // 2) % ny, me % 2
    offsets = peer_offsets(nx, ny)
    right_peer = (me + 1) % nblk
    left_peer = (me + nblk - 1) % nblk
    nsnp = float(snps * nblk)

    def blk_of(d):
        dx, dy, dc = d
        return ((mx + dx) % nx) * (2 * ny) + ((my + dy) % ny) * 2 + (mc + dc) % 2

    barrier = pltpu.get_barrier_semaphore()
    for d in offsets:
        pl.semaphore_signal(barrier, inc=1, device_id={"blk": blk_of(d)}, device_id_type=MESH)
    for dz in range(1, nz):
        pl.semaphore_signal(barrier, inc=1, device_id={"phe": (mz + dz) % nz}, device_id_type=MESH)

    loads = [
        pltpu.make_async_copy(bh_hbm, bh_v, in_sem.at[0]),
        pltpu.make_async_copy(psi_hbm, psi_v, in_sem.at[1]),
        pltpu.make_async_copy(nz_hbm, nz_v, in_sem.at[2]),
        pltpu.make_async_copy(bf_hbm, bf_s, in_sem.at[3]),
        pltpu.make_async_copy(bfr_hbm, bf_v, in_sem.at[4]),
        pltpu.make_async_copy(ss_hbm, ss_v, in_sem.at[5]),
        pltpu.make_async_copy(ld_hbm, ld_v, in_sem.at[6]),
    ]
    for copy in loads:
        copy.start()

    def cols(k):
        return slice(k * LANES, (k + 1) * LANES)

    def as_row(first, second):
        both = jnp.concatenate([first, second], axis=0)
        return jnp.sum(both.T, axis=0, keepdims=True)

    def as_col(row):
        return jnp.broadcast_to(row, (LANES, LANES)).T[:64]

    def remote(src, dst, ssem, rsem, who):
        return pltpu.make_async_remote_copy(src, dst, ssem, rsem, device_id=who, device_id_type=MESH)

    def bytes_wait(ref, sem):
        pltpu.make_async_copy(ref, ref, sem).wait()

    def resid_start(t, row):
        rbuf[t, pl.ds(me, 1)] = row
        for d in offsets:
            slot = rbuf.at[t, pl.ds(me, 1)]
            remote(slot, slot, rs_sem.at[t], rr_sem.at[t], {"blk": blk_of(d)}).start()

    def resid_finish(t):
        bytes_wait(rbuf.at[t, pl.ds(0, nblk - 1)], rr_sem.at[t])
        return jnp.sum(rbuf[t], axis=0, keepdims=True) / nsnp + TINY

    def scale_start(h, rows):
        sbuf[h, pl.ds(2 * me, 2)] = rows
        for d in offsets:
            slot = sbuf.at[h, pl.ds(2 * me, 2)]
            remote(slot, slot, ss_sem.at[h], sr_sem.at[h], {"blk": blk_of(d)}).start()

    def scale_finish(h, amp):
        bytes_wait(sbuf.at[h, pl.ds(0, 2 * nblk - 2)], sr_sem.at[h])
        both = jnp.sum(sbuf[h].reshape(nblk, 2, LANES), axis=0)
        c01, c2 = both[0:1], both[1:2]
        c1 = pltpu.roll(c01, 64, axis=1)
        lane = lax.broadcasted_iota(jnp.int32, (1, LANES), 1)
        total = jnp.where(lane < 64, jnp.maximum(c01 + 2.0 * amp * c1 + amp * amp * c2, 0.0), 0.0)
        mine = jnp.sum(total, axis=1, keepdims=True)
        pbuf[h, pl.ds(mz, 1)] = jnp.broadcast_to(mine, (1, LANES))
        for dz in range(1, nz):
            slot = pbuf.at[h, pl.ds(mz, 1)]
            remote(slot, slot, ps_sem.at[h], pr_sem.at[h], {"phe": (mz + dz) % nz}).start()
        return total

    def phi_finish(h, total):
        bytes_wait(pbuf.at[h, pl.ds(0, nz - 1)], pr_sem.at[h])
        pooled = jnp.sum(pbuf[h], axis=0, keepdims=True) / (nsnp * (64 * nz)) + TINY
        return as_col((total / nsnp + TINY + pooled) / 2.0)

    def coefficients(t, value):
        zero = jnp.zeros((64, LANES), F32)
        c0, c1, c2 = zero, zero, zero
        for k in range(NB):
            s = sh_v[:, cols(k)]
            w = s * s / psi_v[:, cols(k)]
            x = value(k)
            n = nz_v[t, :, cols(k)].astype(F32)
            c0 = c0 + w * x * x
            c1 = c1 + w * x * n
            c2 = c2 + w * n * n
        return jnp.concatenate([as_row(c0, c1), as_row(c2, zero)], axis=0)

    def half(k):
        return k // 2, slice((k % 2) * LANES, (k % 2 + 1) * LANES)

    zero = jnp.zeros((64, LANES), F32)
    loads[0].wait()
    acc = zero
    for k in range(NB):
        b = bh_v[:, cols(k)]
        acc = acc + b * b
    row0 = as_row(acc, zero)
    loads[1].wait()
    loads[2].wait()
    for k in range(NB):
        psi = psi_v[:, cols(k)]
        sh_v[:, cols(k)] = psi / (psi + TINY)
    coef0 = coefficients(0, lambda k: bh_v[:, cols(k)])
    pl.semaphore_wait(barrier, nblk - 1 + nz - 1)
    resid_start(0, row0)
    scale_start(0, coef0)

    early = [
        remote(psi_v, psil_v, ws_sem.at[0], wr_sem.at[0], {"blk": right_peer}),
        remote(psi_v, psir_v, ws_sem.at[1], wr_sem.at[1], {"blk": left_peer}),
        remote(nz_v.at[1], nzl_v, ws_sem.at[2], wr_sem.at[2], {"blk": right_peer}),
        remote(nz_v.at[1], nzr_v, ws_sem.at[3], wr_sem.at[3], {"blk": left_peer}),
    ]
    if EARLY:
        for copy in early:
            copy.start()

    for copy in loads[3:]:
        copy.wait()
    base = me * snps
    sub = lax.broadcasted_iota(jnp.int32, (LANES, snps), 0)
    for i in range(NB):
        rows = slice(i * LANES, (i + 1) * LANES)
        first = bf_s[i * LANES]
        last = bf_s[i * LANES + LANES - 1]
        tile = ld_v[rows, :].astype(F32)
        ra = pltpu.roll(tile, first & (snps - 1), axis=1)
        rb = pltpu.roll(tile, last & (snps - 1), axis=1)
        split = jnp.where(last == first, LANES, last - base - i * LANES)
        rt_m[:, rows] = jnp.where(sub >= split, rb, ra).T.astype(BF16)
    begin = bf_s[0]
    end = bf_s[snps - 1]
    from_left = jnp.where(begin < base, begin & (snps - 1), snps)
    to_right = end & (snps - 1)
    lane = lax.broadcasted_iota(jnp.int32, (64, LANES), 1)

    ss = ss_v[...].astype(F32)
    ss2 = jnp.concatenate([ss, ss], axis=1)

    amp_row = jnp.sqrt(resid_finish(0) * SAMPLE_REF / ss2)
    amp = as_col(amp_row)
    for k in range(NB):
        b = sh_v[:, cols(k)] * (bh_v[:, cols(k)] + amp * nz_v[0, :, cols(k)].astype(F32))
        beta_v[:, cols(k)] = b
        c, w = half(k)
        low_v[c, :, w] = b.astype(BF16)
        x_v[0:64, cols(k)] = b.astype(BF16)
        x_v[64:128, cols(k)] = jnp.where(lane + k * LANES < from_left, b, 0.0).astype(BF16)
        x_v[128:192, cols(k)] = jnp.where(lane + k * LANES >= to_right, b, 0.0).astype(BF16)
    halo = []
    for k in range(NCH):
        kr, kl = NCH - 1 - k, k
        a = remote(low_v.at[kr], lowl_v.at[kr], ls_sem.at[kr], lr_sem.at[kr], {"blk": right_peer})
        b = remote(low_v.at[kl], lowr_v.at[kl], qs_sem.at[kl], qr_sem.at[kl], {"blk": left_peer})
        a.start()
        b.start()
        halo.append((kr, kl, a, b))
    if not EARLY:
        for copy in early:
            copy.start()
    total = scale_finish(0, amp_row)
    acc_v[...] = jnp.dot(x_v[...], rt_m[...], preferred_element_type=F32)
    for kr, kl, a, b in halo:
        a.wait_recv()
        q = lax.broadcasted_iota(jnp.int32, (64, CH), 1)
        x = jnp.where(q + kr * CH >= from_left, lowl_v[kr].astype(F32), 0.0).astype(BF16)
        upto = slice(0, (kr + 1) * CH)
        acc_v[64:128, upto] += jnp.dot(x, rt_m[kr * CH:(kr + 1) * CH, upto], preferred_element_type=F32)
        b.wait_recv()
        x = jnp.where(q + kl * CH < to_right, lowr_v[kl].astype(F32), 0.0).astype(BF16)
        upto = slice(kl * CH, snps)
        acc_v[128:192, upto] += jnp.dot(x, rt_m[kl * CH:(kl + 1) * CH, upto], preferred_element_type=F32)

    def gradient(k):
        first = bf_v[:, cols(k)]
        applied = jnp.where(
            first < base, acc_v[64:128, cols(k)],
            jnp.where(first == end, acc_v[128:192, cols(k)], acc_v[0:64, cols(k)]),
        )
        return bh_v[:, cols(k)] - applied

    racc = zero
    for k in range(NB):
        g = gradient(k)
        racc = racc + g * g
        c, w = half(k)
        t_v[c, :, w] = beta_v[:, cols(k)] + g
    resid_start(1, as_row(racc, zero))

    sums = []
    for k in range(NCH):
        kr, kl = NCH - 1 - k, k
        sums.append(remote(t_v.at[kr], tl_v.at[kr], ts_sem.at[kr], tr_sem.at[kr], {"blk": right_peer}))
        sums.append(remote(t_v.at[kl], tr_v.at[kl], hs_sem.at[kl], hr_sem.at[kl], {"blk": left_peer}))
    for copy in sums:
        copy.start()

    phi = phi_finish(0, total)
    for k in range(NB):
        psi = psi_v[:, cols(k)]
        sh_v[:, cols(k)] = psi / (psi + phi)

    def t_of(k):
        c, w = half(k)
        return t_v[c, :, w]

    scale_start(1, coefficients(1, t_of))
    for copy in early:
        copy.wait_recv()
    for k in range(NB):
        psi = psil_v[:, cols(k)]
        shl_v[:, cols(k)] = psi / (psi + phi)
        psi = psir_v[:, cols(k)]
        shr_v[:, cols(k)] = psi / (psi + phi)

    amp_row = jnp.sqrt(resid_finish(1) * SAMPLE_REF / ss2)
    amp = as_col(amp_row)
    for copy in sums:
        copy.wait_recv()
    for k in range(NB):
        c, w = half(k)
        b = sh_v[:, cols(k)] * (t_v[c, :, w] + amp * nz_v[1, :, cols(k)].astype(F32))
        bl = shl_v[:, cols(k)] * (tl_v[c, :, w] + amp * nzl_v[:, cols(k)].astype(F32))
        br = shr_v[:, cols(k)] * (tr_v[c, :, w] + amp * nzr_v[:, cols(k)].astype(F32))
        beta_v[:, cols(k)] = b
        x_v[0:64, cols(k)] = b.astype(BF16)
        x_v[64:128, cols(k)] = jnp.where(lane + k * LANES < from_left, b, bl).astype(BF16)
        x_v[128:192, cols(k)] = jnp.where(lane + k * LANES >= to_right, b, br).astype(BF16)
    acc_v[...] = jnp.dot(x_v[...], rt_m[...], preferred_element_type=F32)
    racc = zero
    for k in range(NB):
        g = gradient(k)
        racc = racc + g * g
        tail_v[:, cols(k)] = beta_v[:, cols(k)] + g
    resid_start(2, as_row(racc, zero))
    phi = phi_finish(1, scale_finish(1, amp_row))
    for k in range(NB):
        psi = psi_v[:, cols(k)]
        shrink = psi / (psi + phi)
        u_v[:, cols(k)] = shrink * tail_v[:, cols(k)]
        v_v[:, cols(k)] = shrink * nz_v[2, :, cols(k)].astype(F32)

    for t in range(ITERS):
        bytes_wait(rbuf.at[t, pl.ds(0, nblk - 1)], rs_sem.at[t])
    for h in range(ITERS - 1):
        bytes_wait(sbuf.at[h, pl.ds(0, 2 * nblk - 2)], ss_sem.at[h])
        bytes_wait(pbuf.at[h, pl.ds(0, nz - 1)], ps_sem.at[h])
    for copy in early + sums:
        copy.wait_send()
    for kr, kl, a, b in halo:
        a.wait_send()
        b.wait_send()
    amp = as_col(jnp.sqrt(resid_finish(2) * SAMPLE_REF / ss2))
    for k in range(NB):
        out_ref[:, cols(k)] = u_v[:, cols(k)] + amp * v_v[:, cols(k)]


def shards(nx, ny, nz, ld_rows, block_first, beta_hat, psi, noise, sample_size):
    snps = ld_rows.shape[0]
    pheno = beta_hat.shape[0]
    V, dma = pltpu.VMEM, pltpu.SemaphoreType.DMA
    h = ITERS - 1
    nblk = nx * ny * 2
    wide = V((pheno, snps), F32)
    chunks = V((NCH, pheno, CH), F32)
    low = V((NCH, pheno, CH), BF16)
    thin = V((pheno, snps), BF16)
    four = dma((NCH,))
    return pl.pallas_call(
        functools.partial(kernel, nx, ny, nz, snps),
        out_shape=jax.ShapeDtypeStruct((pheno, snps), F32),
        in_specs=[pl.BlockSpec(memory_space=pl.ANY)] * 7,
        out_specs=pl.BlockSpec(memory_space=pltpu.VMEM),
        scratch_shapes=[
            V((snps, snps), BF16), pltpu.SMEM((snps,), jnp.int32), V((1, snps), jnp.int32), wide, wide,
            V((ITERS, pheno, snps), BF16), V((1, pheno), jnp.int32),
            V((snps, snps), BF16), V((3 * pheno, snps), BF16), V((3 * pheno, snps), F32), wide, wide, wide, wide, wide,
            low, low, low, chunks, chunks, chunks, wide, wide, thin, thin, wide, wide,
            V((ITERS, nblk, LANES), F32), V((h, 2 * nblk, LANES), F32), V((h, nz, LANES), F32),
            dma((7,)), dma((ITERS,)), dma((ITERS,)), dma((h,)), dma((h,)), dma((h,)), dma((h,)),
            four, four, four, four, four, four, four, four, four, four,
        ],
        compiler_params=pltpu.CompilerParams(collective_id=0, has_side_effects=True),
        name="shrinkage",
    )(ld_rows, block_first, block_first.reshape(1, snps), beta_hat, psi, noise, sample_size.reshape(1, pheno))


def solution(mesh):
    in_specs = (
        P("blk", None),
        P("blk"),
        P("phe", "blk"),
        P("phe", "blk"),
        P(None, "phe", "blk"),
        P("phe"),
    )
    body = functools.partial(shards, 4, mesh.shape["blk"] // 8, mesh.shape["phe"])
    return jax.shard_map(body, mesh=mesh, in_specs=in_specs, out_specs=P("phe", "blk"), check_vma=False)
```

profile of v0, /device:TPU:1, one launch (start us, length us, event | category | flops | bytes accessed | tf_op | source)
XLA Modules:
  0.0 42.8 jit_solution(5768269239863354331)
XLA Ops:
  0.0 41.1 %shrinkage.1 = f32[64,1024]{1,0:T(8,128)} custom-call(bf16[1024,1024]{1,0:T(8,128)(2,1)} %ld_hbm.1, s32[1024]{0:T(1024)} %bf_hbm.1, s32[1,1024]{1,0:T(1,128)} %bitcast.2, f32[64,1024]{1,0:T(8,128)} %bh_hbm.1, f32[64,1024]{1,0:T(8,128)} %psi_hbm.1, bf16[3,64,1024]{2,1,0:T(8,128)(2,1)} %nz_hbm.1, s32[1,64]{1,0:T(1,128)} %bitcast.3), custom_call_target="tpu_custom_call" | custom-call | tf_op jit(solution)/shard_map/shrinkage/pallas_call | solution.py:319
  41.1 1.7 %copy.8 = f32[64,1024]{1,0:T(8,128)} copy(f32[64,1024]{1,0:T(8,128)} %shrinkage.1) | data formatting | bytes 524288
where the time goes:
time: 43 us; the launch traced here: 42.8 us
  Pallas kernels  41.1 us (96%)
  local copies, waits for them, and re-layouts  1.67 us (4%)
    pallas_call x1, Pallas kernels, shards(): pl.pallas_call(functools.partial(kernel, nx, ny, nz, snps), out_shape=jax...  41.1 us
    unnamed x1, local copies, waits for them, and re-layouts  1.67 us

commit v1 on v0

--- a/solution.py
+++ b/solution.py
@@ -17,7 +17,6 @@
 NCH = 4
 F32 = jnp.float32
 BF16 = jnp.bfloat16
-EARLY = True
 
 
 def peer_offsets(nx, ny):
@@ -36,9 +35,9 @@
     ld_v, bf_s, bf_v, bh_v, psi_v, nz_v, ss_v,
     rt_m, x_v, acc_v, tail_v, beta_v, sh_v, u_v, v_v,
     low_v, lowl_v, lowr_v, t_v, tl_v, tr_v, psil_v, psir_v, nzl_v, nzr_v, shl_v, shr_v,
-    rbuf, sbuf, pbuf,
+    rbuf, sbuf, cbuf, pair_v, pbuf,
     in_sem, rs_sem, rr_sem, ss_sem, sr_sem, ps_sem, pr_sem,
-    ls_sem, lr_sem, qs_sem, qr_sem, ts_sem, tr_sem, ws_sem, wr_sem, hs_sem, hr_sem,
+    ls_sem, lr_sem, qs_sem, qr_sem, ts_sem, tr_sem, ws_sem, wr_sem, hs_sem, hr_sem, cs_sem, go_sem,
 ):
     nblk = nx * ny * 2
     me = lax.axis_index("blk")
@@ -54,10 +53,15 @@
         return ((mx + dx) % nx) * (2 * ny) + ((my + dy) % ny) * 2 + (mc + dc) % 2
 
     barrier = pltpu.get_barrier_semaphore()
+    partner = me + 1 - 2 * mc
     for d in offsets:
-        pl.semaphore_signal(barrier, inc=1, device_id={"blk": blk_of(d)}, device_id_type=MESH)
-    for dz in range(1, nz):
-        pl.semaphore_signal(barrier, inc=1, device_id={"phe": (mz + dz) % nz}, device_id_type=MESH)
+        if d[2] == 0:
+            chip = blk_of(d) // 2
+            pl.semaphore_signal(barrier, inc=1, device_id={"blk": 2 * chip + 1}, device_id_type=MESH)
+
+    @pl.when(mc == 0)
+    def _():
+        pl.semaphore_signal(barrier, inc=1, device_id={"blk": partner}, device_id_type=MESH)
 
     loads = [
         pltpu.make_async_copy(bh_hbm, bh_v, in_sem.at[0]),
@@ -97,15 +101,48 @@
         bytes_wait(rbuf.at[t, pl.ds(0, nblk - 1)], rr_sem.at[t])
         return jnp.sum(rbuf[t], axis=0, keepdims=True) / nsnp + TINY
 
-    def scale_start(h, rows):
-        sbuf[h, pl.ds(2 * me, 2)] = rows
+    def scale_start(rows):
+        sbuf[pl.ds(2 * me, 2)] = rows
         for d in offsets:
-            slot = sbuf.at[h, pl.ds(2 * me, 2)]
-            remote(slot, slot, ss_sem.at[h], sr_sem.at[h], {"blk": blk_of(d)}).start()
+            slot = sbuf.at[pl.ds(2 * me, 2)]
+            remote(slot, slot, ss_sem.at[0], sr_sem.at[0], {"blk": blk_of(d)}).start()
+
+    def paired_start(rows):
+        pair_v[0:2] = rows
+        swap = remote(pair_v.at[0:2], pair_v.at[8:10], cs_sem.at[0], cs_sem.at[1], {"blk": partner})
+        swap.start()
+        swap.wait()
+        mine = me // 2
+        cbuf[pl.ds(2 * mine, 2)] = rows + pair_v[8:10]
+        slot = cbuf.at[pl.ds(2 * mine, 2)]
+
+        def send(chips):
+            for dx, dy in chips:
+                chip = blk_of((dx, dy, 0)) // 2
+                for c in range(2):
+                    remote(slot, slot, ss_sem.at[1], sr_sem.at[1], {"blk": 2 * chip + c}).start()
+
+        chips = [(dx, dy) for dx, dy, dc in offsets if dc == 0]
+        ups = [d for d in chips if d[1] < ny // 2]
+        downs = [d for d in chips if d[1] >= ny // 2]
+
+        @pl.when(mc == 0)
+        def _():
+            send(ups)
+
+        @pl.when(mc == 1)
+        def _():
+            send(downs)
+
+        return 2 * len(ups), 2 * len(downs)
 
     def scale_finish(h, amp):
-        bytes_wait(sbuf.at[h, pl.ds(0, 2 * nblk - 2)], sr_sem.at[h])
-        both = jnp.sum(sbuf[h].reshape(nblk, 2, LANES), axis=0)
+        if h == 0:
+            bytes_wait(sbuf.at[pl.ds(0, 2 * nblk - 2)], sr_sem.at[h])
+            both = jnp.sum(sbuf[...].reshape(nblk, 2, LANES), axis=0)
+        else:
+            bytes_wait(cbuf.at[pl.ds(0, nblk - 2)], sr_sem.at[h])
+            both = jnp.sum(cbuf[...].reshape(nblk // 2, 2, LANES), axis=0)
         c01, c2 = both[0:1], both[1:2]
         c1 = pltpu.roll(c01, 64, axis=1)
         lane = lax.broadcasted_iota(jnp.int32, (1, LANES), 1)
@@ -151,9 +188,23 @@
         psi = psi_v[:, cols(k)]
         sh_v[:, cols(k)] = psi / (psi + TINY)
     coef0 = coefficients(0, lambda k: bh_v[:, cols(k)])
-    pl.semaphore_wait(barrier, nblk - 1 + nz - 1)
+    @pl.when(mc == 1)
+    def _():
+        pl.semaphore_wait(barrier, nblk - 1)
+        pl.semaphore_signal(go_sem, inc=1, device_id={"blk": partner}, device_id_type=MESH)
+
+    @pl.when(mc == 0)
+    def _():
+        pl.semaphore_wait(go_sem, 1)
+
     resid_start(0, row0)
-    scale_start(0, coef0)
+
+    @pl.when(mc == 0)
+    def _():
+        for dz in range(1, nz):
+            pl.semaphore_signal(barrier, inc=1, device_id={"phe": (mz + dz) % nz}, device_id_type=MESH)
+
+    scale_start(coef0)
 
     early = [
         remote(psi_v, psil_v, ws_sem.at[0], wr_sem.at[0], {"blk": right_peer}),
@@ -161,9 +212,8 @@
         remote(nz_v.at[1], nzl_v, ws_sem.at[2], wr_sem.at[2], {"blk": right_peer}),
         remote(nz_v.at[1], nzr_v, ws_sem.at[3], wr_sem.at[3], {"blk": left_peer}),
     ]
-    if EARLY:
-        for copy in early:
-            copy.start()
+    for copy in early[2:]:
+        copy.start()
 
     for copy in loads[3:]:
         copy.wait()
@@ -205,9 +255,18 @@
         a.start()
         b.start()
         halo.append((kr, kl, a, b))
-    if not EARLY:
-        for copy in early:
-            copy.start()
+    for copy in early[:2]:
+        copy.start()
+
+    @pl.when(mc == 0)
+    def _():
+        pl.semaphore_wait(barrier, nz - 1)
+        pl.semaphore_signal(go_sem, inc=1, device_id={"blk": partner}, device_id_type=MESH)
+
+    @pl.when(mc == 1)
+    def _():
+        pl.semaphore_wait(go_sem, 1)
+
     total = scale_finish(0, amp_row)
     acc_v[...] = jnp.dot(x_v[...], rt_m[...], preferred_element_type=F32)
     for kr, kl, a, b in halo:
@@ -254,7 +313,7 @@
         c, w = half(k)
         return t_v[c, :, w]
 
-    scale_start(1, coefficients(1, t_of))
+    n_ups, n_downs = paired_start(coefficients(1, t_of))
     for copy in early:
         copy.wait_recv()
     for k in range(NB):
@@ -293,8 +352,17 @@
     for t in range(ITERS):
         bytes_wait(rbuf.at[t, pl.ds(0, nblk - 1)], rs_sem.at[t])
     for h in range(ITERS - 1):
-        bytes_wait(sbuf.at[h, pl.ds(0, 2 * nblk - 2)], ss_sem.at[h])
         bytes_wait(pbuf.at[h, pl.ds(0, nz - 1)], ps_sem.at[h])
+    bytes_wait(sbuf.at[pl.ds(0, 2 * nblk - 2)], ss_sem.at[0])
+
+    @pl.when(mc == 0)
+    def _():
+        bytes_wait(sbuf.at[pl.ds(0, 2 * n_ups)], ss_sem.at[1])
+
+    @pl.when(mc == 1)
+    def _():
+        bytes_wait(sbuf.at[pl.ds(0, 2 * n_downs)], ss_sem.at[1])
+
     for copy in early + sums:
         copy.wait_send()
     for kr, kl, a, b in halo:
@@ -316,9 +384,10 @@
     low = V((NCH, pheno, CH), BF16)
     thin = V((pheno, snps), BF16)
     four = dma((NCH,))
+    arrays = (ld_rows, block_first, block_first.reshape(1, snps), beta_hat, psi, noise, sample_size.reshape(1, pheno))
     return pl.pallas_call(
         functools.partial(kernel, nx, ny, nz, snps),
-        out_shape=jax.ShapeDtypeStruct((pheno, snps), F32),
+        out_shape=pltpu.VMEM((pheno, snps), F32),
         in_specs=[pl.BlockSpec(memory_space=pl.ANY)] * 7,
         out_specs=pl.BlockSpec(memory_space=pltpu.VMEM),
         scratch_shapes=[
@@ -326,13 +395,14 @@
             V((ITERS, pheno, snps), BF16), V((1, pheno), jnp.int32),
             V((snps, snps), BF16), V((3 * pheno, snps), BF16), V((3 * pheno, snps), F32), wide, wide, wide, wide, wide,
             low, low, low, chunks, chunks, chunks, wide, wide, thin, thin, wide, wide,
-            V((ITERS, nblk, LANES), F32), V((h, 2 * nblk, LANES), F32), V((h, nz, LANES), F32),
+            V((ITERS, nblk, LANES), F32), V((2 * nblk, LANES), F32), V((nblk, LANES), F32),
+            V((16, LANES), F32), V((h, nz, LANES), F32),
             dma((7,)), dma((ITERS,)), dma((ITERS,)), dma((h,)), dma((h,)), dma((h,)), dma((h,)),
-            four, four, four, four, four, four, four, four, four, four,
+            four, four, four, four, four, four, four, four, four, four, dma((2,)), pltpu.SemaphoreType.REGULAR,
         ],
-        compiler_params=pltpu.CompilerParams(collective_id=0, has_side_effects=True),
+        compiler_params=pltpu.CompilerParams(collective_id=0, has_side_effects=True, vmem_limit_bytes=32 * 1024 * 1024),
         name="shrinkage",
-    )(ld_rows, block_first, block_first.reshape(1, snps), beta_hat, psi, noise, sample_size.reshape(1, pheno))
+    )(*[pltpu.with_memory_space_constraint(a, pltpu.HBM) for a in arrays])
 
 
 def solution(mesh):

time: 43 us -> 40.7 us (0.947)
  Pallas kernels: 41.1 us -> 39.9 us
  local copies, waits for them, and re-layouts: 1.67 us -> 0.71 us
    pallas_call x1, Pallas kernels: 41.1 us -> 39.9 us  [shards(): pl.pallas_call(functools.partial(kernel, nx, ny, nz, snps), out_shape=plt...]
    unnamed x1, local copies, waits for them, and re-layouts: 1.67 us -> 0.71 us
where the time goes in v1:
time: 40.7 us; the launch traced here: 40.6 us
  Pallas kernels  39.9 us (98%)
  local copies, waits for them, and re-layouts  0.71 us (2%)
    pallas_call x1, Pallas kernels, shards(): pl.pallas_call(functools.partial(kernel, nx, ny, nz, snps), out_shape=plt...  39.9 us

profile of v1, /device:TPU:1, one launch (start us, length us, event | category | flops | bytes accessed | tf_op | source)
XLA Modules:
  0.0 40.6 jit_solution(1168656356750633579)
XLA Ops:
  0.0 39.9 %shrinkage.1 = f32[64,1024]{1,0:T(8,128)S(1)} custom-call(bf16[1024,1024]{1,0:T(8,128)(2,1)} %ld_hbm.1, s32[1024]{0:T(1024)} %bf_hbm.1, s32[1,1024]{1,0:T(1,128)} %bitcast.2, f32[64,1024]{1,0:T(8,128)} %bh_hbm.1, f32[64,1024]{1,0:T(8,128)} %psi_hbm.1, bf16[3,64,1024]{2,1,0:T(8,128)(2,1)} %nz_hbm.1, s32[1,64]{1,0:T(1,128)} %bitcast.3), custom_call_target="tpu_custom_call" | custom-call | tf_op jit(solution)/shard_map/shrinkage/pallas_call | solution.py:388
  39.9 0.7 %copy.8 = f32[64,1024]{1,0:T(8,128)} copy(f32[64,1024]{1,0:T(8,128)S(1)} %shrinkage.1) | data formatting | bytes 524288

commit v2 on v0

--- a/solution.py
+++ b/solution.py
@@ -17,7 +17,6 @@
 NCH = 4
 F32 = jnp.float32
 BF16 = jnp.bfloat16
-EARLY = True
 
 
 def peer_offsets(nx, ny):
@@ -36,9 +35,9 @@
     ld_v, bf_s, bf_v, bh_v, psi_v, nz_v, ss_v,
     rt_m, x_v, acc_v, tail_v, beta_v, sh_v, u_v, v_v,
     low_v, lowl_v, lowr_v, t_v, tl_v, tr_v, psil_v, psir_v, nzl_v, nzr_v, shl_v, shr_v,
-    rbuf, sbuf, pbuf,
+    rbuf, sbuf, pbuf, total_v,
     in_sem, rs_sem, rr_sem, ss_sem, sr_sem, ps_sem, pr_sem,
-    ls_sem, lr_sem, qs_sem, qr_sem, ts_sem, tr_sem, ws_sem, wr_sem, hs_sem, hr_sem,
+    ls_sem, lr_sem, qs_sem, qr_sem, ts_sem, tr_sem, ws_sem, wr_sem, hs_sem, hr_sem, go_sem,
 ):
     nblk = nx * ny * 2
     me = lax.axis_index("blk")
@@ -54,10 +53,17 @@
         return ((mx + dx) % nx) * (2 * ny) + ((my + dy) % ny) * 2 + (mc + dc) % 2
 
     barrier = pltpu.get_barrier_semaphore()
+    partner = me + 1 - 2 * mc
+    not_first = me > 0
+    not_last = me < nblk - 1
     for d in offsets:
-        pl.semaphore_signal(barrier, inc=1, device_id={"blk": blk_of(d)}, device_id_type=MESH)
-    for dz in range(1, nz):
-        pl.semaphore_signal(barrier, inc=1, device_id={"phe": (mz + dz) % nz}, device_id_type=MESH)
+        if d[2] == 0:
+            chip = blk_of(d) // 2
+            pl.semaphore_signal(barrier, inc=1, device_id={"blk": 2 * chip}, device_id_type=MESH)
+
+    @pl.when(mc == 1)
+    def _():
+        pl.semaphore_signal(barrier, inc=1, device_id={"blk": partner}, device_id_type=MESH)
 
     loads = [
         pltpu.make_async_copy(bh_hbm, bh_v, in_sem.at[0]),
@@ -87,34 +93,46 @@
     def bytes_wait(ref, sem):
         pltpu.make_async_copy(ref, ref, sem).wait()
 
+    def to_all(ref, ssem, rsem):
+        for d in offsets:
+            remote(ref, ref, ssem, rsem, {"blk": blk_of(d)}).start()
+
     def resid_start(t, row):
         rbuf[t, pl.ds(me, 1)] = row
-        for d in offsets:
-            slot = rbuf.at[t, pl.ds(me, 1)]
-            remote(slot, slot, rs_sem.at[t], rr_sem.at[t], {"blk": blk_of(d)}).start()
+        to_all(rbuf.at[t, pl.ds(me, 1)], rs_sem.at[t], rr_sem.at[t])
 
     def resid_finish(t):
         bytes_wait(rbuf.at[t, pl.ds(0, nblk - 1)], rr_sem.at[t])
-        return jnp.sum(rbuf[t], axis=0, keepdims=True) / nsnp + TINY
+        return amplitude(jnp.sum(rbuf[t], axis=0, keepdims=True))
+
+    def amplitude(total):
+        return jnp.sqrt((total / nsnp + TINY) * SAMPLE_REF / ss2)
 
     def scale_start(h, rows):
         sbuf[h, pl.ds(2 * me, 2)] = rows
-        for d in offsets:
-            slot = sbuf.at[h, pl.ds(2 * me, 2)]
-            remote(slot, slot, ss_sem.at[h], sr_sem.at[h], {"blk": blk_of(d)}).start()
-
-    def scale_finish(h, amp):
+        to_all(sbuf.at[h, pl.ds(2 * me, 2)], ss_sem.at[h], sr_sem.at[h])
+
+    def scale_sums(h):
         bytes_wait(sbuf.at[h, pl.ds(0, 2 * nblk - 2)], sr_sem.at[h])
-        both = jnp.sum(sbuf[h].reshape(nblk, 2, LANES), axis=0)
-        c01, c2 = both[0:1], both[1:2]
-        c1 = pltpu.roll(c01, 64, axis=1)
+        return jnp.sum(sbuf[h].reshape(nblk, 2, LANES), axis=0)
+
+    def scale_finish(h, both, amp):
+        c0 = pltpu.roll(both[0:1], 64, axis=1)
+        c1 = both[1:2]
+        c2 = pltpu.roll(both[1:2], 64, axis=1)
         lane = lax.broadcasted_iota(jnp.int32, (1, LANES), 1)
-        total = jnp.where(lane < 64, jnp.maximum(c01 + 2.0 * amp * c1 + amp * amp * c2, 0.0), 0.0)
+        total = jnp.where(lane < 64, jnp.maximum(c0 + 2.0 * amp * c1 + amp * amp * c2, 0.0), 0.0)
         mine = jnp.sum(total, axis=1, keepdims=True)
         pbuf[h, pl.ds(mz, 1)] = jnp.broadcast_to(mine, (1, LANES))
-        for dz in range(1, nz):
+
+        @pl.when(mc == 1)
+        def _():
             slot = pbuf.at[h, pl.ds(mz, 1)]
-            remote(slot, slot, ps_sem.at[h], pr_sem.at[h], {"phe": (mz + dz) % nz}).start()
+            for blk in (partner, me):
+                for dz in sorted(range(1, nz), key=lambda d: -min(d, nz - d)):
+                    who = {"blk": blk, "phe": (mz + dz) % nz}
+                    remote(slot, slot, ps_sem.at[h], pr_sem.at[h], who).start()
+
         return total
 
     def phi_finish(h, total):
@@ -122,7 +140,7 @@
         pooled = jnp.sum(pbuf[h], axis=0, keepdims=True) / (nsnp * (64 * nz)) + TINY
         return as_col((total / nsnp + TINY + pooled) / 2.0)
 
-    def coefficients(t, value):
+    def coefficients(t, value, resid):
         zero = jnp.zeros((64, LANES), F32)
         c0, c1, c2 = zero, zero, zero
         for k in range(NB):
@@ -133,10 +151,42 @@
             c0 = c0 + w * x * x
             c1 = c1 + w * x * n
             c2 = c2 + w * n * n
-        return jnp.concatenate([as_row(c0, c1), as_row(c2, zero)], axis=0)
+        return jnp.concatenate([as_row(resid, c0), as_row(c1, c2)], axis=0)
+
+    def start_both(rights, lefts):
+        @pl.when(not_last)
+        def _():
+            for copy in rights:
+                copy.start()
+
+        @pl.when(not_first)
+        def _():
+            for copy in lefts:
+                copy.start()
+
+    def wait_both(rights, lefts):
+        @pl.when(not_first)
+        def _():
+            for copy in rights:
+                copy.wait_recv()
+
+        @pl.when(not_last)
+        def _():
+            for copy in lefts:
+                copy.wait_recv()
 
     def half(k):
         return k // 2, slice((k % 2) * LANES, (k % 2 + 1) * LANES)
+
+    @pl.when(me == 0)
+    def _():
+        for ref in (lowl_v, tl_v, psil_v, nzl_v):
+            ref[...] = jnp.zeros_like(ref) if ref is not psil_v else jnp.ones_like(ref)
+
+    @pl.when(me == nblk - 1)
+    def _():
+        for ref in (lowr_v, tr_v, psir_v, nzr_v):
+            ref[...] = jnp.zeros_like(ref) if ref is not psir_v else jnp.ones_like(ref)
 
     zero = jnp.zeros((64, LANES), F32)
     loads[0].wait()
@@ -144,16 +194,27 @@
     for k in range(NB):
         b = bh_v[:, cols(k)]
         acc = acc + b * b
-    row0 = as_row(acc, zero)
     loads[1].wait()
     loads[2].wait()
     for k in range(NB):
         psi = psi_v[:, cols(k)]
         sh_v[:, cols(k)] = psi / (psi + TINY)
-    coef0 = coefficients(0, lambda k: bh_v[:, cols(k)])
-    pl.semaphore_wait(barrier, nblk - 1 + nz - 1)
-    resid_start(0, row0)
-    scale_start(0, coef0)
+    rows = coefficients(0, lambda k: bh_v[:, cols(k)], acc)
+    @pl.when(mc == 0)
+    def _():
+        pl.semaphore_wait(barrier, nblk - 1)
+        pl.semaphore_signal(go_sem, inc=1, device_id={"blk": partner}, device_id_type=MESH)
+
+    @pl.when(mc == 1)
+    def _():
+        pl.semaphore_wait(go_sem, 1)
+
+    scale_start(0, rows)
+
+    @pl.when(mc == 1)
+    def _():
+        for dz in range(1, nz):
+            pl.semaphore_signal(barrier, inc=1, device_id={"phe": (mz + dz) % nz}, device_id_type=MESH)
 
     early = [
         remote(psi_v, psil_v, ws_sem.at[0], wr_sem.at[0], {"blk": right_peer}),
@@ -161,9 +222,7 @@
         remote(nz_v.at[1], nzl_v, ws_sem.at[2], wr_sem.at[2], {"blk": right_peer}),
         remote(nz_v.at[1], nzr_v, ws_sem.at[3], wr_sem.at[3], {"blk": left_peer}),
     ]
-    if EARLY:
-        for copy in early:
-            copy.start()
+    start_both(early[2:3], early[3:4])
 
     for copy in loads[3:]:
         copy.wait()
@@ -181,42 +240,49 @@
     begin = bf_s[0]
     end = bf_s[snps - 1]
     from_left = jnp.where(begin < base, begin & (snps - 1), snps)
-    to_right = end & (snps - 1)
+    to_right = jnp.where(not_last, end & (snps - 1), 0)
     lane = lax.broadcasted_iota(jnp.int32, (64, LANES), 1)
 
     ss = ss_v[...].astype(F32)
     ss2 = jnp.concatenate([ss, ss], axis=1)
 
-    amp_row = jnp.sqrt(resid_finish(0) * SAMPLE_REF / ss2)
+    both = scale_sums(0)
+    amp_row = amplitude(both[0:1])
     amp = as_col(amp_row)
-    for k in range(NB):
-        b = sh_v[:, cols(k)] * (bh_v[:, cols(k)] + amp * nz_v[0, :, cols(k)].astype(F32))
-        beta_v[:, cols(k)] = b
-        c, w = half(k)
-        low_v[c, :, w] = b.astype(BF16)
-        x_v[0:64, cols(k)] = b.astype(BF16)
-        x_v[64:128, cols(k)] = jnp.where(lane + k * LANES < from_left, b, 0.0).astype(BF16)
-        x_v[128:192, cols(k)] = jnp.where(lane + k * LANES >= to_right, b, 0.0).astype(BF16)
     halo = []
     for k in range(NCH):
         kr, kl = NCH - 1 - k, k
         a = remote(low_v.at[kr], lowl_v.at[kr], ls_sem.at[kr], lr_sem.at[kr], {"blk": right_peer})
         b = remote(low_v.at[kl], lowr_v.at[kl], qs_sem.at[kl], qr_sem.at[kl], {"blk": left_peer})
-        a.start()
-        b.start()
         halo.append((kr, kl, a, b))
-    if not EARLY:
-        for copy in early:
-            copy.start()
-    total = scale_finish(0, amp_row)
+    for k, (kr, kl, a, b) in enumerate(halo):
+        if k < NCH // 2:
+            for j in (2 * kr, 2 * kr + 1, 2 * kl, 2 * kl + 1):
+                v = sh_v[:, cols(j)] * (bh_v[:, cols(j)] + amp * nz_v[0, :, cols(j)].astype(F32))
+                beta_v[:, cols(j)] = v
+                c, w = half(j)
+                low_v[c, :, w] = v.astype(BF16)
+        start_both([a], [b])
+    start_both(early[0:1], early[1:2])
+
+    @pl.when(mc == 1)
+    def _():
+        pl.semaphore_wait(barrier, nz - 1)
+
+    total = scale_finish(0, both, amp_row)
+    for k in range(NB):
+        v = beta_v[:, cols(k)]
+        x_v[0:64, cols(k)] = v.astype(BF16)
+        x_v[64:128, cols(k)] = jnp.where(lane + k * LANES < from_left, v, 0.0).astype(BF16)
+        x_v[128:192, cols(k)] = jnp.where(lane + k * LANES >= to_right, v, 0.0).astype(BF16)
     acc_v[...] = jnp.dot(x_v[...], rt_m[...], preferred_element_type=F32)
     for kr, kl, a, b in halo:
-        a.wait_recv()
+        wait_both([a], [])
         q = lax.broadcasted_iota(jnp.int32, (64, CH), 1)
         x = jnp.where(q + kr * CH >= from_left, lowl_v[kr].astype(F32), 0.0).astype(BF16)
         upto = slice(0, (kr + 1) * CH)
         acc_v[64:128, upto] += jnp.dot(x, rt_m[kr * CH:(kr + 1) * CH, upto], preferred_element_type=F32)
-        b.wait_recv()
+        wait_both([], [b])
         x = jnp.where(q + kl * CH < to_right, lowr_v[kl].astype(F32), 0.0).astype(BF16)
         upto = slice(kl * CH, snps)
         acc_v[128:192, upto] += jnp.dot(x, rt_m[kl * CH:(kl + 1) * CH, upto], preferred_element_type=F32)
@@ -235,15 +301,19 @@
         racc = racc + g * g
         c, w = half(k)
         t_v[c, :, w] = beta_v[:, cols(k)] + g
-    resid_start(1, as_row(racc, zero))
+    resid_start(0, as_row(racc, zero))
 
     sums = []
     for k in range(NCH):
         kr, kl = NCH - 1 - k, k
         sums.append(remote(t_v.at[kr], tl_v.at[kr], ts_sem.at[kr], tr_sem.at[kr], {"blk": right_peer}))
         sums.append(remote(t_v.at[kl], tr_v.at[kl], hs_sem.at[kl], hr_sem.at[kl], {"blk": left_peer}))
-    for copy in sums:
-        copy.start()
+
+    late = mz >= nz // 2
+
+    @pl.when(jnp.logical_not(late))
+    def _():
+        start_both(sums[0::2], sums[1::2])
 
     phi = phi_finish(0, total)
     for k in range(NB):
@@ -254,19 +324,27 @@
         c, w = half(k)
         return t_v[c, :, w]
 
-    scale_start(1, coefficients(1, t_of))
-    for copy in early:
-        copy.wait_recv()
+    scale_start(1, coefficients(1, t_of, zero))
+
+    @pl.when(late)
+    def _():
+        start_both(sums[0::2], sums[1::2])
+
+    wait_both(early[0::2], early[1::2])
     for k in range(NB):
         psi = psil_v[:, cols(k)]
         shl_v[:, cols(k)] = psi / (psi + phi)
         psi = psir_v[:, cols(k)]
         shr_v[:, cols(k)] = psi / (psi + phi)
 
-    amp_row = jnp.sqrt(resid_finish(1) * SAMPLE_REF / ss2)
+    amp_row = resid_finish(0)
     amp = as_col(amp_row)
-    for copy in sums:
-        copy.wait_recv()
+
+    @pl.when(late)
+    def _():
+        total_v[...] = scale_finish(1, scale_sums(1), amp_row)
+
+    wait_both(sums[0::2], sums[1::2])
     for k in range(NB):
         c, w = half(k)
         b = sh_v[:, cols(k)] * (t_v[c, :, w] + amp * nz_v[1, :, cols(k)].astype(F32))
@@ -282,25 +360,40 @@
         g = gradient(k)
         racc = racc + g * g
         tail_v[:, cols(k)] = beta_v[:, cols(k)] + g
-    resid_start(2, as_row(racc, zero))
-    phi = phi_finish(1, scale_finish(1, amp_row))
+    resid_start(1, as_row(racc, zero))
+
+    @pl.when(jnp.logical_not(late))
+    def _():
+        total_v[...] = scale_finish(1, scale_sums(1), amp_row)
+
+    phi = phi_finish(1, total_v[...])
     for k in range(NB):
         psi = psi_v[:, cols(k)]
         shrink = psi / (psi + phi)
         u_v[:, cols(k)] = shrink * tail_v[:, cols(k)]
         v_v[:, cols(k)] = shrink * nz_v[2, :, cols(k)].astype(F32)
 
-    for t in range(ITERS):
-        bytes_wait(rbuf.at[t, pl.ds(0, nblk - 1)], rs_sem.at[t])
     for h in range(ITERS - 1):
+        bytes_wait(rbuf.at[h, pl.ds(0, nblk - 1)], rs_sem.at[h])
         bytes_wait(sbuf.at[h, pl.ds(0, 2 * nblk - 2)], ss_sem.at[h])
-        bytes_wait(pbuf.at[h, pl.ds(0, nz - 1)], ps_sem.at[h])
-    for copy in early + sums:
-        copy.wait_send()
-    for kr, kl, a, b in halo:
-        a.wait_send()
-        b.wait_send()
-    amp = as_col(jnp.sqrt(resid_finish(2) * SAMPLE_REF / ss2))
+
+    @pl.when(mc == 1)
+    def _():
+        for h in range(ITERS - 1):
+            for _ in range(2):
+                bytes_wait(pbuf.at[h, pl.ds(0, nz - 1)], ps_sem.at[h])
+
+    @pl.when(not_last)
+    def _():
+        for copy in early[0::2] + sums[0::2] + [a for _, _, a, _ in halo]:
+            copy.wait_send()
+
+    @pl.when(not_first)
+    def _():
+        for copy in early[1::2] + sums[1::2] + [b for _, _, _, b in halo]:
+            copy.wait_send()
+
+    amp = as_col(resid_finish(1))
     for k in range(NB):
         out_ref[:, cols(k)] = u_v[:, cols(k)] + amp * v_v[:, cols(k)]
 
@@ -316,9 +409,10 @@
     low = V((NCH, pheno, CH), BF16)
     thin = V((pheno, snps), BF16)
     four = dma((NCH,))
+    arrays = (ld_rows, block_first, block_first.reshape(1, snps), beta_hat, psi, noise, sample_size.reshape(1, pheno))
     return pl.pallas_call(
         functools.partial(kernel, nx, ny, nz, snps),
-        out_shape=jax.ShapeDtypeStruct((pheno, snps), F32),
+        out_shape=pltpu.VMEM((pheno, snps), F32),
         in_specs=[pl.BlockSpec(memory_space=pl.ANY)] * 7,
         out_specs=pl.BlockSpec(memory_space=pltpu.VMEM),
         scratch_shapes=[
@@ -326,13 +420,14 @@
             V((ITERS, pheno, snps), BF16), V((1, pheno), jnp.int32),
             V((snps, snps), BF16), V((3 * pheno, snps), BF16), V((3 * pheno, snps), F32), wide, wide, wide, wide, wide,
             low, low, low, chunks, chunks, chunks, wide, wide, thin, thin, wide, wide,
-            V((ITERS, nblk, LANES), F32), V((h, 2 * nblk, LANES), F32), V((h, nz, LANES), F32),
-            dma((7,)), dma((ITERS,)), dma((ITERS,)), dma((h,)), dma((h,)), dma((h,)), dma((h,)),
-            four, four, four, four, four, four, four, four, four, four,
+            V((h, nblk, LANES), F32), V((h, 2 * nblk, LANES), F32), V((h, nz, LANES), F32),
+            V((1, LANES), F32),
+            dma((7,)), dma((h,)), dma((h,)), dma((h,)), dma((h,)), dma((h,)), dma((h,)),
+            four, four, four, four, four, four, four, four, four, four, pltpu.SemaphoreType.REGULAR,
         ],
-        compiler_params=pltpu.CompilerParams(collective_id=0, has_side_effects=True),
+        compiler_params=pltpu.CompilerParams(collective_id=0, has_side_effects=True, vmem_limit_bytes=32 * 1024 * 1024),
         name="shrinkage",
-    )(ld_rows, block_first, block_first.reshape(1, snps), beta_hat, psi, noise, sample_size.reshape(1, pheno))
+    )(*[pltpu.with_memory_space_constraint(a, pltpu.HBM) for a in arrays])
 
 
 def solution(mesh):

time: 43 us -> 38.2 us (0.89)
  Pallas kernels: 41.1 us -> 37.3 us
  local copies, waits for them, and re-layouts: 1.67 us -> 0.71 us
    pallas_call x1, Pallas kernels: 41.1 us -> 37.3 us  [shards(): pl.pallas_call(functools.partial(kernel, nx, ny, nz, snps), out_shape=plt...]
    unnamed x1, local copies, waits for them, and re-layouts: 1.67 us -> 0.71 us
where the time goes in v2:
time: 38.2 us; the launch traced here: 38 us
  Pallas kernels  37.3 us (98%)
  local copies, waits for them, and re-layouts  0.71 us (2%)
    pallas_call x1, Pallas kernels, shards(): pl.pallas_call(functools.partial(kernel, nx, ny, nz, snps), out_shape=plt...  37.3 us

profile of v2, /device:TPU:1, one launch (start us, length us, event | category | flops | bytes accessed | tf_op | source)
XLA Modules:
  0.0 38.0 jit_solution(4935537194839003806)
XLA Ops:
  0.0 37.3 %shrinkage.1 = f32[64,1024]{1,0:T(8,128)S(1)} custom-call(bf16[1024,1024]{1,0:T(8,128)(2,1)} %ld_hbm.1, s32[1024]{0:T(1024)} %bf_hbm.1, s32[1,1024]{1,0:T(1,128)} %bitcast.2, f32[64,1024]{1,0:T(8,128)} %bh_hbm.1, f32[64,1024]{1,0:T(8,128)} %psi_hbm.1, bf16[3,64,1024]{2,1,0:T(8,128)(2,1)} %nz_hbm.1, s32[1,64]{1,0:T(1,128)} %bitcast.3), custom_call_target="tpu_custom_call" | custom-call | tf_op jit(solution)/shard_map/shrinkage/pallas_call | solution.py:413
  37.3 0.7 %copy.8 = f32[64,1024]{1,0:T(8,128)} copy(f32[64,1024]{1,0:T(8,128)S(1)} %shrinkage.1) | data formatting | bytes 524288

commit v3 on v2

--- a/solution.py
+++ b/solution.py
@@ -35,7 +35,7 @@
     ld_v, bf_s, bf_v, bh_v, psi_v, nz_v, ss_v,
     rt_m, x_v, acc_v, tail_v, beta_v, sh_v, u_v, v_v,
     low_v, lowl_v, lowr_v, t_v, tl_v, tr_v, psil_v, psir_v, nzl_v, nzr_v, shl_v, shr_v,
-    rbuf, sbuf, pbuf, total_v,
+    rbuf, sbuf, pbuf, scale_v, amp_v,
     in_sem, rs_sem, rr_sem, ss_sem, sr_sem, ps_sem, pr_sem,
     ls_sem, lr_sem, qs_sem, qr_sem, ts_sem, tr_sem, ws_sem, wr_sem, hs_sem, hr_sem, go_sem,
 ):
@@ -54,6 +54,8 @@
 
     barrier = pltpu.get_barrier_semaphore()
     partner = me + 1 - 2 * mc
+    late = mz >= nz // 2
+    ahead = jnp.logical_not(late)
     not_first = me > 0
     not_last = me < nblk - 1
     for d in offsets:
@@ -133,12 +135,12 @@
                     who = {"blk": blk, "phe": (mz + dz) % nz}
                     remote(slot, slot, ps_sem.at[h], pr_sem.at[h], who).start()
 
-        return total
-
-    def phi_finish(h, total):
+        scale_v[...] = as_col(total / nsnp + TINY)
+
+    def phi_finish(h):
         bytes_wait(pbuf.at[h, pl.ds(0, nz - 1)], pr_sem.at[h])
         pooled = jnp.sum(pbuf[h], axis=0, keepdims=True) / (nsnp * (64 * nz)) + TINY
-        return as_col((total / nsnp + TINY + pooled) / 2.0)
+        return (scale_v[...] + pooled) / 2.0
 
     def coefficients(t, value, resid):
         zero = jnp.zeros((64, LANES), F32)
@@ -255,6 +257,13 @@
         a = remote(low_v.at[kr], lowl_v.at[kr], ls_sem.at[kr], lr_sem.at[kr], {"blk": right_peer})
         b = remote(low_v.at[kl], lowr_v.at[kl], qs_sem.at[kl], qr_sem.at[kl], {"blk": left_peer})
         halo.append((kr, kl, a, b))
+    def pool():
+        @pl.when(mc == 1)
+        def _():
+            pl.semaphore_wait(barrier, nz - 1)
+
+        scale_finish(0, both, amp_row)
+
     for k, (kr, kl, a, b) in enumerate(halo):
         if k < NCH // 2:
             for j in (2 * kr, 2 * kr + 1, 2 * kl, 2 * kl + 1):
@@ -263,13 +272,11 @@
                 c, w = half(j)
                 low_v[c, :, w] = v.astype(BF16)
         start_both([a], [b])
+        if k == 0:
+            pl.when(late)(pool)
     start_both(early[0:1], early[1:2])
-
-    @pl.when(mc == 1)
-    def _():
-        pl.semaphore_wait(barrier, nz - 1)
-
-    total = scale_finish(0, both, amp_row)
+    pl.when(ahead)(pool)
+
     for k in range(NB):
         v = beta_v[:, cols(k)]
         x_v[0:64, cols(k)] = v.astype(BF16)
@@ -301,7 +308,6 @@
         racc = racc + g * g
         c, w = half(k)
         t_v[c, :, w] = beta_v[:, cols(k)] + g
-    resid_start(0, as_row(racc, zero))
 
     sums = []
     for k in range(NCH):
@@ -309,13 +315,12 @@
         sums.append(remote(t_v.at[kr], tl_v.at[kr], ts_sem.at[kr], tr_sem.at[kr], {"blk": right_peer}))
         sums.append(remote(t_v.at[kl], tr_v.at[kl], hs_sem.at[kl], hr_sem.at[kl], {"blk": left_peer}))
 
-    late = mz >= nz // 2
-
-    @pl.when(jnp.logical_not(late))
-    def _():
+    @pl.when(ahead)
+    def _():
+        resid_start(0, as_row(racc, zero))
         start_both(sums[0::2], sums[1::2])
 
-    phi = phi_finish(0, total)
+    phi = phi_finish(0)
     for k in range(NB):
         psi = psi_v[:, cols(k)]
         sh_v[:, cols(k)] = psi / (psi + phi)
@@ -324,7 +329,7 @@
         c, w = half(k)
         return t_v[c, :, w]
 
-    scale_start(1, coefficients(1, t_of, zero))
+    scale_start(1, coefficients(1, t_of, racc))
 
     @pl.when(late)
     def _():
@@ -337,13 +342,18 @@
         psi = psir_v[:, cols(k)]
         shr_v[:, cols(k)] = psi / (psi + phi)
 
-    amp_row = resid_finish(0)
+    @pl.when(ahead)
+    def _():
+        amp_v[...] = resid_finish(0)
+
+    @pl.when(late)
+    def _():
+        both = scale_sums(1)
+        amp_v[...] = amplitude(both[0:1])
+        scale_finish(1, both, amp_v[...])
+
+    amp_row = amp_v[...]
     amp = as_col(amp_row)
-
-    @pl.when(late)
-    def _():
-        total_v[...] = scale_finish(1, scale_sums(1), amp_row)
-
     wait_both(sums[0::2], sums[1::2])
     for k in range(NB):
         c, w = half(k)
@@ -362,40 +372,58 @@
         tail_v[:, cols(k)] = beta_v[:, cols(k)] + g
     resid_start(1, as_row(racc, zero))
 
-    @pl.when(jnp.logical_not(late))
-    def _():
-        total_v[...] = scale_finish(1, scale_sums(1), amp_row)
-
-    phi = phi_finish(1, total_v[...])
-    for k in range(NB):
-        psi = psi_v[:, cols(k)]
-        shrink = psi / (psi + phi)
-        u_v[:, cols(k)] = shrink * tail_v[:, cols(k)]
-        v_v[:, cols(k)] = shrink * nz_v[2, :, cols(k)].astype(F32)
-
-    for h in range(ITERS - 1):
-        bytes_wait(rbuf.at[h, pl.ds(0, nblk - 1)], rs_sem.at[h])
-        bytes_wait(sbuf.at[h, pl.ds(0, 2 * nblk - 2)], ss_sem.at[h])
-
-    @pl.when(mc == 1)
-    def _():
+    def drain():
+        @pl.when(ahead)
+        def _():
+            bytes_wait(rbuf.at[0, pl.ds(0, nblk - 1)], rs_sem.at[0])
+
+        bytes_wait(rbuf.at[1, pl.ds(0, nblk - 1)], rs_sem.at[1])
         for h in range(ITERS - 1):
-            for _ in range(2):
-                bytes_wait(pbuf.at[h, pl.ds(0, nz - 1)], ps_sem.at[h])
-
-    @pl.when(not_last)
-    def _():
-        for copy in early[0::2] + sums[0::2] + [a for _, _, a, _ in halo]:
-            copy.wait_send()
-
-    @pl.when(not_first)
-    def _():
-        for copy in early[1::2] + sums[1::2] + [b for _, _, _, b in halo]:
-            copy.wait_send()
-
-    amp = as_col(resid_finish(1))
-    for k in range(NB):
-        out_ref[:, cols(k)] = u_v[:, cols(k)] + amp * v_v[:, cols(k)]
+            bytes_wait(sbuf.at[h, pl.ds(0, 2 * nblk - 2)], ss_sem.at[h])
+
+        @pl.when(mc == 1)
+        def _():
+            for h in range(ITERS - 1):
+                for _ in range(2):
+                    bytes_wait(pbuf.at[h, pl.ds(0, nz - 1)], ps_sem.at[h])
+
+        @pl.when(not_last)
+        def _():
+            for copy in early[0::2] + sums[0::2] + [a for _, _, a, _ in halo]:
+                copy.wait_send()
+
+        @pl.when(not_first)
+        def _():
+            for copy in early[1::2] + sums[1::2] + [b for _, _, _, b in halo]:
+                copy.wait_send()
+
+    def noise_of(k):
+        return nz_v[ITERS - 1, :, cols(k)].astype(F32)
+
+    @pl.when(ahead)
+    def _():
+        scale_finish(1, scale_sums(1), amp_row)
+        amp = as_col(resid_finish(1))
+        for k in range(NB):
+            u_v[:, cols(k)] = tail_v[:, cols(k)] + amp * noise_of(k)
+        drain()
+        phi = phi_finish(1)
+        for k in range(NB):
+            psi = psi_v[:, cols(k)]
+            out_ref[:, cols(k)] = psi / (psi + phi) * u_v[:, cols(k)]
+
+    @pl.when(late)
+    def _():
+        phi = phi_finish(1)
+        for k in range(NB):
+            psi = psi_v[:, cols(k)]
+            shrink = psi / (psi + phi)
+            u_v[:, cols(k)] = shrink * tail_v[:, cols(k)]
+            v_v[:, cols(k)] = shrink * noise_of(k)
+        drain()
+        amp = as_col(resid_finish(1))
+        for k in range(NB):
+            out_ref[:, cols(k)] = u_v[:, cols(k)] + amp * v_v[:, cols(k)]
 
 
 def shards(nx, ny, nz, ld_rows, block_first, beta_hat, psi, noise, sample_size):
@@ -421,7 +449,7 @@
             V((snps, snps), BF16), V((3 * pheno, snps), BF16), V((3 * pheno, snps), F32), wide, wide, wide, wide, wide,
             low, low, low, chunks, chunks, chunks, wide, wide, thin, thin, wide, wide,
             V((h, nblk, LANES), F32), V((h, 2 * nblk, LANES), F32), V((h, nz, LANES), F32),
-            V((1, LANES), F32),
+            V((pheno, LANES), F32), V((1, LANES), F32),
             dma((7,)), dma((h,)), dma((h,)), dma((h,)), dma((h,)), dma((h,)), dma((h,)),
             four, four, four, four, four, four, four, four, four, four, pltpu.SemaphoreType.REGULAR,
         ],

time: 38.2 us -> 37.8 us (0.990)
  no operation moved by 1% of the time
where the time goes in v3:
time: 37.8 us; the launch traced here: 37.7 us
  Pallas kernels  37 us (98%)
  local copies, waits for them, and re-layouts  0.71 us (2%)
    pallas_call x1, Pallas kernels, shards(): pl.pallas_call(functools.partial(kernel, nx, ny, nz, snps), out_shape=plt...  37 us

profile of v3, /device:TPU:1, one launch (start us, length us, event | category | flops | bytes accessed | tf_op | source)
XLA Modules:
  0.0 37.7 jit_solution(7099820941489726342)
XLA Ops:
  0.0 37.0 %shrinkage.1 = f32[64,1024]{1,0:T(8,128)S(1)} custom-call(bf16[1024,1024]{1,0:T(8,128)(2,1)} %ld_hbm.1, s32[1024]{0:T(1024)} %bf_hbm.1, s32[1,1024]{1,0:T(1,128)} %bitcast.2, f32[64,1024]{1,0:T(8,128)} %bh_hbm.1, f32[64,1024]{1,0:T(8,128)} %psi_hbm.1, bf16[3,64,1024]{2,1,0:T(8,128)(2,1)} %nz_hbm.1, s32[1,64]{1,0:T(1,128)} %bitcast.3), custom_call_target="tpu_custom_call" | custom-call | tf_op jit(solution)/shard_map/shrinkage/pallas_call | solution.py:441
  37.0 0.7 %copy.8 = f32[64,1024]{1,0:T(8,128)} copy(f32[64,1024]{1,0:T(8,128)S(1)} %shrinkage.1) | data formatting | bytes 524288

commit v4 on v3

--- a/solution.py
+++ b/solution.py
@@ -130,8 +130,8 @@
         @pl.when(mc == 1)
         def _():
             slot = pbuf.at[h, pl.ds(mz, 1)]
-            for blk in (partner, me):
-                for dz in sorted(range(1, nz), key=lambda d: -min(d, nz - d)):
+            for dz in sorted(range(1, nz), key=lambda d: -min(d, nz - d)):
+                for blk in (partner, me):
                     who = {"blk": blk, "phe": (mz + dz) % nz}
                     remote(slot, slot, ps_sem.at[h], pr_sem.at[h], who).start()
 
@@ -202,6 +202,8 @@
         psi = psi_v[:, cols(k)]
         sh_v[:, cols(k)] = psi / (psi + TINY)
     rows = coefficients(0, lambda k: bh_v[:, cols(k)], acc)
+    sbuf[0, pl.ds(2 * me, 2)] = rows
+
     @pl.when(mc == 0)
     def _():
         pl.semaphore_wait(barrier, nblk - 1)
@@ -211,7 +213,7 @@
     def _():
         pl.semaphore_wait(go_sem, 1)
 
-    scale_start(0, rows)
+    to_all(sbuf.at[0, pl.ds(2 * me, 2)], ss_sem.at[0], sr_sem.at[0])
 
     @pl.when(mc == 1)
     def _():

time: 37.8 us -> 37.8 us (level)
  no operation moved by 1% of the time
where the time goes in v4:
time: 37.8 us; the launch traced here: 37.7 us
  Pallas kernels  37 us (98%)
  local copies, waits for them, and re-layouts  0.71 us (2%)
    pallas_call x1, Pallas kernels, shards(): pl.pallas_call(functools.partial(kernel, nx, ny, nz, snps), out_shape=plt...  37 us

profile of v4, /device:TPU:1, one launch (start us, length us, event | category | flops | bytes accessed | tf_op | source)
XLA Modules:
  0.0 37.7 jit_solution(16208897643248279736)
XLA Ops:
  0.0 37.0 %shrinkage.1 = f32[64,1024]{1,0:T(8,128)S(1)} custom-call(bf16[1024,1024]{1,0:T(8,128)(2,1)} %ld_hbm.1, s32[1024]{0:T(1024)} %bf_hbm.1, s32[1,1024]{1,0:T(1,128)} %bitcast.2, f32[64,1024]{1,0:T(8,128)} %bh_hbm.1, f32[64,1024]{1,0:T(8,128)} %psi_hbm.1, bf16[3,64,1024]{2,1,0:T(8,128)(2,1)} %nz_hbm.1, s32[1,64]{1,0:T(1,128)} %bitcast.3), custom_call_target="tpu_custom_call" | custom-call | tf_op jit(solution)/shard_map/shrinkage/pallas_call | solution.py:443
  37.0 0.7 %copy.8 = f32[64,1024]{1,0:T(8,128)} copy(f32[64,1024]{1,0:T(8,128)S(1)} %shrinkage.1) | data formatting | bytes 524288
